TPU v7x, 32 devices: a whole 2x2x4 slice. The times are simulated.
32 devices in a mesh: grp: 4 (over z), seq: 8 (over y, x, core).
Axes of the slice: x: 2, y: 2, z: 4, core: 2. Of those that a mesh axis runs over, the one named last changes fastest.
Arguments:
- hidden_in: bfloat16 [24, 4096], P(None, ('grp', 'seq')), may hold values from -6 to 6
- norm_gain: float32 [4096], replicated, may hold values from 0.5 to 1.5
- w_ssm_in: bfloat16 [4096, 8192], P(None, ('grp', 'seq')), may hold values from -0.09375 to 0.09375
- w_ssm_gate: bfloat16 [4096, 8192], P(None, ('grp', 'seq')), may hold values from -0.09375 to 0.09375
- conv_weight: float32 [4, 8192], P(None, ('grp', 'seq')), may hold values from -3 to 3
- conv_bias: float32 [8192], P(('grp', 'seq')), may hold values from -0.5 to 0.5
- conv_state: bfloat16 [24, 3, 8192], P(None, None, ('grp', 'seq')), may hold values from -6 to 6
- w_state_proj: bfloat16 [8192, 288], P(('grp', 'seq')), may hold values from -0.0625 to 0.0625
- w_step: bfloat16 [256, 8192], P(None, ('grp', 'seq')), may hold values from -0.375 to 0.375
- step_bias: float32 [8192], P(('grp', 'seq')), may hold values from -4 to -1
- log_decay: float32 [16, 8192], P(None, ('grp', 'seq')), may hold values from 0 to 2.7
- skip_gain: float32 [8192], P(('grp', 'seq')), may hold values from 0.5 to 1.5
- ssm_state: float32 [24, 16, 8192], P(None, None, ('grp', 'seq')), may hold values from -6 to 6
- w_ssm_out: bfloat16 [8192, 4096], P(('grp', 'seq')), may hold values from -0.125 to 0.125
- w_query: bfloat16 [4096, 2048], P(None, 'grp'), may hold values from -6 to 6
- key_projection: bfloat16 [4096, 1024], P(None, 'grp'), may hold values from -0.09375 to 0.09375
- value_projection: bfloat16 [4096, 1024], P(None, 'grp'), may hold values from -0.09375 to 0.09375
- w_attn_out: bfloat16 [2048, 4096], P('grp', 'seq'), may hold values from -0.125 to 0.125
- w_mlp_gate: bfloat16 [4096, 14336], P(None, ('grp', 'seq')), may hold values from -0.09375 to 0.09375
- w_mlp_up: bfloat16 [4096, 14336], P(None, ('grp', 'seq')), may hold values from -0.09375 to 0.09375
- w_mlp_down: bfloat16 [14336, 4096], P(('grp', 'seq')), may hold values from -0.09375 to 0.09375
- cached_inputs: bfloat16 [24, 512, 4096], P('seq'), may hold values from -6 to 6
- window_lengths: int32 [24], replicated, may hold values from 1 to 512, as said below
Outputs:
- hidden_out: bfloat16 [24, 4096], P(None, ('grp', 'seq'))
- state_out: float32 [24, 16, 8192], P(None, None, ('grp', 'seq'))
Inputs may be any that keep to these rules, and one draw needn't show every extreme that they name: `window_lengths`: every sequence has at least one valid cached position, and some sequence fills the whole window of 512.
All inputs are finite; a program needn't handle non-finite values.
Results may differ from a plain program's by a relative error of at most 0.012.
The roundings to bfloat16 on the way count: a program that leaves them out, or rounds other values in their place, can miss the bound.
Values may be sent and summed in bfloat16 or wider, within the bound.
No kernel may reach another device: no remote copies, remote signals or barrier semaphores. Data moves between devices by JAX's collectives and lax.ppermute only.
A program may use at most 128 MiB of HBM per device.

v0:
```python
import jax
import jax.numpy as jnp
from jax import lax
from jax.sharding import PartitionSpec as P

HEAD_SIZE = 128


epsilon = 1e-05
rope_base = 10000.0


def apply_rotary(head_values, positions):
    half_dim = head_values.shape[-1] // 2
    frequency = rope_base ** (
        -(jnp.arange(half_dim, dtype=jnp.float32) * 2.0) / head_values.shape[-1]
    )
    angles = positions[..., None, None] * frequency
    cosine = jnp.cos(angles)
    sine_part = jnp.sin(angles)
    front_half = head_values[..., :half_dim]
    back_half = head_values[..., half_dim:]
    return jnp.concatenate(
        [front_half * cosine - back_half * sine_part, back_half * cosine + front_half * sine_part],
        axis=-1,
    )


def per_device(
    hidden_in,
    norm_gain,
    w_ssm_in,
    w_ssm_gate,
    conv_weight,
    conv_bias,
    conv_state,
    w_state_proj,
    w_step,
    step_bias,
    log_decay,
    skip_gain,
    ssm_state,
    w_ssm_out,
    w_query,
    key_projection,
    value_projection,
    w_attn_out,
    w_mlp_gate,
    w_mlp_up,
    w_mlp_down,
    cached_inputs,
    window_lengths,
):
    batch_rows = hidden_in.shape[0]
    model_width = norm_gain.shape[0]
    hidden_f = hidden_in.astype(jnp.float32)
    raw_full = lax.all_gather(hidden_in, ("grp", "seq"), axis=1, tiled=True).astype(jnp.float32)
    row_scale = lax.rsqrt(jnp.mean(raw_full * raw_full, axis=1, keepdims=True) + epsilon)
    normed_input = (raw_full * row_scale * norm_gain).astype(jnp.bfloat16)
    ssm_input = jnp.dot(normed_input, w_ssm_in, preferred_element_type=jnp.float32).astype(
        jnp.bfloat16
    )
    gate_input = jnp.dot(normed_input, w_ssm_gate, preferred_element_type=jnp.float32)
    past_inputs = conv_state.astype(jnp.float32)
    conv_sum = (
        conv_bias
        + jnp.sum(past_inputs * conv_weight[:-1][None], axis=1)
        + conv_weight[-1] * lax.optimization_barrier(ssm_input).astype(jnp.float32)
    )
    conv_out = jax.nn.silu(conv_sum)
    rank_size = w_step.shape[0]
    state_size = log_decay.shape[0]
    low_rank = lax.psum(
        jnp.dot(conv_out.astype(jnp.bfloat16), w_state_proj, preferred_element_type=jnp.float32),
        ("grp", "seq"),
    )
    step_low = low_rank[:, :rank_size].astype(jnp.bfloat16)
    input_map = low_rank[:, rank_size : rank_size + state_size]
    output_map = low_rank[:, rank_size + state_size :]
    step_size = jax.nn.softplus(
        jnp.dot(step_low, w_step, preferred_element_type=jnp.float32) + step_bias
    )
    decay_rate = jnp.exp(log_decay)
    state_out = (
        jnp.exp(-step_size[:, None, :] * decay_rate[None]) * ssm_state
        + step_size[:, None, :] * input_map[:, :, None] * conv_out[:, None, :]
    )
    ssm_mixed = jnp.sum(state_out * output_map[:, :, None], axis=1) + skip_gain * conv_out
    ssm_gated = (ssm_mixed * jax.nn.silu(gate_input)).astype(jnp.bfloat16)
    ssm_term = jnp.dot(ssm_gated, w_ssm_out, preferred_element_type=jnp.float32)
    ssm_summed = lax.psum_scatter(ssm_term, ("grp", "seq"), scatter_dimension=1, tiled=True)
    gate_act = jnp.dot(normed_input, w_mlp_gate, preferred_element_type=jnp.float32)
    up_act = jnp.dot(normed_input, w_mlp_up, preferred_element_type=jnp.float32)
    mlp_hidden = (jax.nn.silu(gate_act) * up_act).astype(jnp.bfloat16)
    mlp_term = jnp.dot(mlp_hidden, w_mlp_down, preferred_element_type=jnp.float32)
    own_seqs = cached_inputs.shape[0]
    window_size = cached_inputs.shape[1]
    seq_start = lax.axis_index("seq") * own_seqs
    normed_own = lax.dynamic_slice_in_dim(normed_input, seq_start, own_seqs, 0)
    lengths_own = lax.dynamic_slice_in_dim(window_lengths, seq_start, own_seqs, 0)
    heads_here = w_query.shape[1] // HEAD_SIZE
    kv_here = key_projection.shape[1] // HEAD_SIZE
    heads_per_group = heads_here // kv_here
    attention_scale = HEAD_SIZE ** (-0.5)
    fresh_position = lengths_own.astype(jnp.float32)
    query = apply_rotary(
        jnp.dot(normed_own, w_query, preferred_element_type=jnp.float32).reshape(
            own_seqs, heads_here, HEAD_SIZE
        ),
        fresh_position,
    ).astype(jnp.bfloat16)
    fresh_key = apply_rotary(
        jnp.dot(normed_own, key_projection, preferred_element_type=jnp.float32).reshape(
            own_seqs, kv_here, HEAD_SIZE
        ),
        fresh_position,
    ).astype(jnp.bfloat16)
    fresh_value = (
        jnp.dot(normed_own, value_projection, preferred_element_type=jnp.float32)
        .astype(jnp.bfloat16)
        .reshape(own_seqs, kv_here, HEAD_SIZE)
    )
    flat_inputs = cached_inputs.reshape(own_seqs * window_size, model_width)
    slot_ids = jnp.arange(window_size, dtype=jnp.int32)
    positions = jnp.broadcast_to(slot_ids[None, :], (own_seqs, window_size)).astype(jnp.float32)
    window_key_rows = jnp.dot(
        flat_inputs, key_projection, preferred_element_type=jnp.float32
    ).reshape(own_seqs, window_size, kv_here, HEAD_SIZE)
    window_key_rows = apply_rotary(window_key_rows, positions).astype(jnp.bfloat16)
    window_value_rows = (
        jnp.dot(flat_inputs, value_projection, preferred_element_type=jnp.float32)
        .astype(jnp.bfloat16)
        .reshape(own_seqs, window_size, kv_here, HEAD_SIZE)
    )
    grouped_query = query.astype(jnp.float32).reshape(own_seqs, kv_here, heads_per_group, HEAD_SIZE)
    scores = (
        jnp.einsum("bkgd,bpkd->bkgp", grouped_query, window_key_rows.astype(jnp.float32))
        * attention_scale
    )
    fresh_score = (
        jnp.einsum("ynow,ynw->yno", grouped_query, fresh_key.astype(jnp.float32)) * attention_scale
    )
    is_valid = (slot_ids[None, :] < lengths_own[:, None])[:, None, None, :]
    scores = jnp.where(is_valid, scores, -1e30)
    joint_max = jnp.maximum(jnp.max(scores, axis=-1), fresh_score)
    weights = jnp.where(is_valid, jnp.exp(scores - joint_max[..., None]), 0.0)
    weight_new = jnp.exp(fresh_score - joint_max)
    joint_total = jnp.sum(weights, axis=-1) + weight_new
    joint_sum = (
        jnp.einsum("bkgp,bpkd->bkgd", weights, window_value_rows.astype(jnp.float32))
        + weight_new[..., None] * fresh_value.astype(jnp.float32)[:, :, None, :]
    )
    attended_own = (
        (joint_sum / joint_total[..., None])
        .reshape(own_seqs, heads_here * HEAD_SIZE)
        .astype(jnp.bfloat16)
    )
    attended = lax.all_gather(attended_own, "seq", axis=0, tiled=True)
    attn_cols = jnp.dot(attended, w_attn_out, preferred_element_type=jnp.float32)
    col_start = lax.axis_index("seq") * w_attn_out.shape[1]
    attn_term = lax.dynamic_update_slice(
        jnp.zeros((batch_rows, model_width), jnp.float32), attn_cols, (jnp.int32(0), col_start)
    )
    other_terms = mlp_term + attn_term
    summed = ssm_summed + lax.psum_scatter(
        other_terms, ("grp", "seq"), scatter_dimension=1, tiled=True
    )
    hidden_out = (hidden_f + summed).astype(jnp.bfloat16)
    return (hidden_out, state_out)


def solution(mesh):
    placed = (
        P(None, ("grp", "seq")),
        P(),
        P(None, ("grp", "seq")),
        P(None, ("grp", "seq")),
        P(None, ("grp", "seq")),
        P(("grp", "seq")),
        P(None, None, ("grp", "seq")),
        P(("grp", "seq"), None),
        P(None, ("grp", "seq")),
        P(("grp", "seq")),
        P(None, ("grp", "seq")),
        P(("grp", "seq")),
        P(None, None, ("grp", "seq")),
        P(("grp", "seq"), None),
        P(None, "grp"),
        P(None, "grp"),
        P(None, "grp"),
        P("grp", "seq"),
        P(None, ("grp", "seq")),
        P(None, ("grp", "seq")),
        P(("grp", "seq"), None),
        P("seq", None, None),
        P(),
    )
    return jax.shard_map(
        per_device,
        mesh=mesh,
        in_specs=placed,
        out_specs=(P(None, ("grp", "seq")), P(None, None, ("grp", "seq"))),
        check_vma=False,
    )
```

profile of v0, /device:TPU:0, one launch (start us, length us, event | category | flops | bytes accessed | tf_op | source)
XLA Modules:
  0.0 289.1 jit_solution(317169863830582743)
XLA Ops:
  7.3 44.2 %all_gather.6 = bf16[24,4096]{1,0:T(8,128)(2,1)S(1)} all-gather(bf16[24,128]{1,0:T(8,128)(2,1)} %param.23), channel_id=1, replica_groups=mesh['grp'=4,'seq'=8] {'grp','seq'}, dimensions={1}, use_global_device_ids=true | all-gather | bytes 202752 | tf_op jit(solution)/shard_map/all_gather | solution.py:57
  51.4 0.2 fusion.13
  51.6 0.8 fusion.15
  52.5 2.8 fusion.25
  55.3 0.1 fusion.42
  55.5 0.1 multiply_cosine_fusion.1
  55.6 0.5 multiply_cosine_fusion
  56.1 2.0 fusion.23
  58.1 4.1 %copy.38 = bf16[256,4096]{1,0:T(8,128)(2,1)} copy(bf16[256,4096]{0,1:T(8,128)(2,1)} %bitcast.38) | data formatting | bytes 4194304 | tf_op jit(solution)/shard_map/dot_general | solution.py:126
  62.3 0.1 subtract_convert_fusion.2
  62.3 7.1 %fusion = f32[3,512,2,128]{1,3,2,0:T(8,128)S(1)} fusion(bf16[2,128,4096,1]{2,1,0,3:T(8,128)(2,1)} %bitcast.39, bf16[3,512,4096]{2,1,0:T(8,128)(2,1)} %param.44), kind=kOutput, calls=%fused_computation | convolution fusion | flops 3221225472 | bytes 16252928 | tf_op jit(solution)/shard_map/dot_general | solution.py:126
  69.5 0.1 maximum_bitcast_fusion
  69.6 0.3 subtract_convert_fusion
  69.9 0.2 fusion.32
  70.1 0.3 fusion.44
  70.5 0.2 fusion.31
  70.7 0.4 fusion.8
  71.1 7.4 %convolution_convert_fusion = bf16[1536,256]{1,0:T(8,128)(2,1)} fusion(bf16[1536,4096]{1,0:T(8,128)(2,1)} %bitcast.48, bf16[4096,256]{1,0:T(8,128)(2,1)S(1)} %copy-done), kind=kOutput, calls=%fused_computation.3 | convolution fusion | flops 3221618688 | bytes 15466496 | tf_op jit(solution)/shard_map/dot_general | solution.py:131
  78.4 2.0 reshape.155
  80.5 0.3 fusion.7
  80.8 7.0 %all-gather = bf16[8,3,512]{2,1,0:T(4,128)(2,1)S(1)} all-gather(bf16[1,3,512]{2,1,0:T(4,128)(2,1)S(1)} %reshape.157), channel_id=1, replica_groups=mesh['grp'=4,'seq'=8] {'seq'}, dimensions={0}, use_global_device_ids=true | all-gather | bytes 27648 | tf_op jit(solution)/shard_map/all_gather | solution.py:158
  87.8 3.1 %fusion.48 = f32[24,448]{1,0:T(8,128)S(1)} fusion(bf16[24,4096]{1,0:T(8,128)(2,1)S(1)} %fusion.15, bf16[4096,448]{0,1:T(8,128)(2,1)} %param.41), kind=kOutput, calls=%fused_computation.85 | convolution fusion | flops 88080384 | bytes 3909632 | tf_op jit(solution)/shard_map/dot_general | solution.py:92
  91.0 2.1 convolution_convert_fusion.1
  93.2 0.2 fusion.28
  93.4 38.3 %psum.7 = f32[24,288]{1,0:T(8,128)S(1)} all-reduce(f32[24,288]{1,0:T(8,128)S(1)} %fusion.28), channel_id=1, replica_groups=mesh['grp'=4,'seq'=8] {'grp','seq'}, use_global_device_ids=true, to_apply=%region_2.3 | all-reduce | flops 6912 | bytes 55296 | tf_op jit(solution)/shard_map/psum | solution.py:73
  131.8 0.2 fusion.45
  132.0 5.1 %fusion.4 = f32[24,4096]{1,0:T(8,128)S(1)} fusion(bf16[448,4096]{1,0:T(8,128)(2,1)} %param.43, bf16[24,4096]{1,0:T(8,128)(2,1)S(1)} %fusion.15, bf16[4096,448]{0,1:T(8,128)(2,1)} %param.42, f32[24,448]{1,0:T(8,128)S(1)} %fusion.48), kind=kOutput, calls=%fused_computation.8 | convolution fusion | flops 176225280 | bytes 7972864 | tf_op jit(solution)/shard_map/dot_general | solution.py:95
  137.1 0.2 fusion.2
  137.3 1.9 multiply_reduce_fusion
  139.3 4.3 %convolution_add_fusion = f32[24,4096]{1,0:T(8,128)} fusion(f32[24,4096]{1,0:T(8,128)S(1)} %fusion.2, bf16[256,4096]{1,0:T(8,128)(2,1)} %param.36, f32[24,256]{1,0:T(8,128)S(1)} %get-tuple-element.2, f32[24,256]{1,0:T(8,128)S(1)} %divide_multiply_fusion, f32[256]{0:T(256)S(1)} %copy-done.10, bf16[24,4096]{1,0:T(8,128)(2,1)S(1)} %fusion.15, ...), kind=kOutput, calls=%fused_computation.2 | convolution fusion | flops 100810752 | bytes 5227520 | tf_op jit(solution)/shard_map/dot_general | solution.py:90
  143.6 137.4 %reduce-scatter.2.cloned.1.call-done = f32[24,128]{1,0:T(8,128)} async-done(((f32[24,4096]{1,0:T(8,128)}), f32[24,128]{1,0:T(8,128)}) %reduce-scatter.2.cloned.1.call-update) | async-done | bytes 12304 | tf_op jit(solution)/shard_map/reduce_scatter | solution.py:91
  280.9 1.3 add_convert_fusion.1
  (43 shorter events, 0.6 us)
Async XLA Ops:
  7.2 63.5 %copy-start = (bf16[4096,256]{1,0:T(8,128)(2,1)S(1)}, bf16[4096,256]{1,0:T(8,128)(2,1)}, u32[]{:S(2)}) copy-start(bf16[4096,256]{1,0:T(8,128)(2,1)} %param.39) | copy-start | bytes 6291460
  7.2 273.8 %reduce-scatter.2.cloned.1.call-start = ((), (), s32[]{:S(2)}) async-start(), calls=%async_computation.1 | async-start | bytes 405504 | tf_op jit(solution)/shard_map/reduce_scatter | solution.py:91
  52.4 2.9 copy-start.11
  90.9 2.2 copy-start.7
  90.9 2.2 copy-start.4
  91.0 2.2 copy-start.8
  91.0 2.2 copy-start.2
  91.0 40.8 %copy-start.6 = (f32[16,256]{1,0:T(8,128)S(1)}, f32[16,256]{1,0:T(8,128)}, u32[]{:S(2)}) copy-start(f32[16,256]{1,0:T(8,128)} %param.33) | copy-start | bytes 49156
  91.0 40.8 %copy-start.3 = (bf16[256,256]{1,0:T(8,128)(2,1)S(1)}, bf16[256,256]{1,0:T(8,128)(2,1)}, u32[]{:S(2)}) copy-start(bf16[256,256]{1,0:T(8,128)(2,1)} %param.31) | copy-start | bytes 393220
  91.0 40.8 %copy-start.9 = (f32[256]{0:T(256)S(1)}, f32[256]{0:T(256)}, u32[]{:S(2)}) copy-start(f32[256]{0:T(256)} %param.32) | copy-start | bytes 3076
  132.0 5.1 %copy-start.1 = (bf16[512,512]{1,0:T(8,128)(2,1)S(1)}, bf16[512,512]{1,0:T(8,128)(2,1)}, u32[]{:S(2)}) copy-start(bf16[512,512]{1,0:T(8,128)(2,1)} %param.40) | copy-start | bytes 1572868
  132.0 7.2 %copy-start.10 = (f32[256]{0:T(256)S(1)}, f32[256]{0:T(256)}, u32[]{:S(2)}) copy-start(f32[256]{0:T(256)} %param.34) | copy-start | bytes 3076
  139.3 141.7 %copy-start.5 = (bf16[24,128]{1,0:T(8,128)(2,1)S(1)}, bf16[24,128]{1,0:T(8,128)(2,1)}, u32[]{:S(2)}) copy-start(bf16[24,128]{1,0:T(8,128)(2,1)} %param.23) | copy-start | bytes 18436
Sparse Core Ops, SparseCore 0:
  143.7 137.2 reduce-scatter.1
where the time goes:
time: 290 us; the launch traced here: 289 us
  waiting for transfers between devices  137 us (47%)
  blocking collectives  89.5 us (31%)
  matrix products  35.6 us (12%)
  between operations  14.3 us (5%)
  local copies, waits for them, and re-layouts  6.37 us (2%)
  other arithmetic  5.87 us (2%)
    reduce_scatter x1, waiting for transfers between devices, per_device(): lax.psum_scatter(ssm_term, ('grp', 'seq'), scatter_dimension=1, tiled=True)  137 us
    all_gather x1, blocking collectives, per_device(): lax.all_gather(hidden_in, ('grp', 'seq'), axis=1, tiled=True)  44.2 us
    psum x1, blocking collectives, per_device(): lax.psum(jnp.dot(conv_out.astype(jnp.bfloat16), w_state_proj, preferred_e...  38.3 us
    dot_general x1, matrix products, per_device(): jnp.dot(flat_inputs, value_projection, preferred_element_type=jnp.float32)  7.38 us
    dot_general x1, matrix products, per_device(): jnp.dot(flat_inputs, key_projection, preferred_element_type=jnp.float32)  7.13 us
    all_gather x1, blocking collectives, per_device(): attended = lax.all_gather(attended_own, 'seq', axis=0, tiled=True)  7.02 us
  transfers between devices with their start and end apart: 1, of which 1 were waited for; matrix products, arithmetic and copies ran while one was open for 0% of the time, Pallas kernels for 0%

commit v1 on v0

--- a/solution.py
+++ b/solution.py
@@ -24,6 +24,31 @@
         [front_half * cosine - back_half * sine_part, back_half * cosine + front_half * sine_part],
         axis=-1,
     )
+
+
+BOTH = ("grp", "seq")
+
+
+def gather_features(own):
+    count = lax.axis_size(BOTH)
+    rows = jnp.broadcast_to(own[None], (count,) + own.shape)
+    blocks = lax.all_to_all(rows, BOTH, 0, 0)
+    return blocks.transpose(1, 0, 2).reshape(own.shape[0], count * own.shape[1])
+
+
+def exchange_sum(value):
+    count = lax.axis_size(BOTH)
+    step = 1
+    while step < count:
+        value = value + lax.ppermute(value, BOTH, [(i, i ^ step) for i in range(count)])
+        step *= 2
+    return value
+
+
+def scatter_sum(term):
+    count = lax.axis_size(BOTH)
+    blocks = term.astype(jnp.bfloat16).reshape(term.shape[0], count, term.shape[1] // count)
+    return jnp.sum(lax.all_to_all(blocks, BOTH, 1, 1).astype(jnp.float32), axis=1)
 
 
 def per_device(
@@ -54,7 +79,7 @@
     batch_rows = hidden_in.shape[0]
     model_width = norm_gain.shape[0]
     hidden_f = hidden_in.astype(jnp.float32)
-    raw_full = lax.all_gather(hidden_in, ("grp", "seq"), axis=1, tiled=True).astype(jnp.float32)
+    raw_full = gather_features(hidden_in).astype(jnp.float32)
     row_scale = lax.rsqrt(jnp.mean(raw_full * raw_full, axis=1, keepdims=True) + epsilon)
     normed_input = (raw_full * row_scale * norm_gain).astype(jnp.bfloat16)
     ssm_input = jnp.dot(normed_input, w_ssm_in, preferred_element_type=jnp.float32).astype(
@@ -70,9 +95,8 @@
     conv_out = jax.nn.silu(conv_sum)
     rank_size = w_step.shape[0]
     state_size = log_decay.shape[0]
-    low_rank = lax.psum(
-        jnp.dot(conv_out.astype(jnp.bfloat16), w_state_proj, preferred_element_type=jnp.float32),
-        ("grp", "seq"),
+    low_rank = exchange_sum(
+        jnp.dot(conv_out.astype(jnp.bfloat16), w_state_proj, preferred_element_type=jnp.float32)
     )
     step_low = low_rank[:, :rank_size].astype(jnp.bfloat16)
     input_map = low_rank[:, rank_size : rank_size + state_size]
@@ -88,7 +112,6 @@
     ssm_mixed = jnp.sum(state_out * output_map[:, :, None], axis=1) + skip_gain * conv_out
     ssm_gated = (ssm_mixed * jax.nn.silu(gate_input)).astype(jnp.bfloat16)
     ssm_term = jnp.dot(ssm_gated, w_ssm_out, preferred_element_type=jnp.float32)
-    ssm_summed = lax.psum_scatter(ssm_term, ("grp", "seq"), scatter_dimension=1, tiled=True)
     gate_act = jnp.dot(normed_input, w_mlp_gate, preferred_element_type=jnp.float32)
     up_act = jnp.dot(normed_input, w_mlp_up, preferred_element_type=jnp.float32)
     mlp_hidden = (jax.nn.silu(gate_act) * up_act).astype(jnp.bfloat16)
@@ -155,16 +178,16 @@
         .reshape(own_seqs, heads_here * HEAD_SIZE)
         .astype(jnp.bfloat16)
     )
-    attended = lax.all_gather(attended_own, "seq", axis=0, tiled=True)
+    seq_count = lax.axis_size("seq")
+    attended = lax.all_to_all(
+        jnp.broadcast_to(attended_own[None], (seq_count,) + attended_own.shape), "seq", 0, 0
+    ).reshape(batch_rows, heads_here * HEAD_SIZE)
     attn_cols = jnp.dot(attended, w_attn_out, preferred_element_type=jnp.float32)
     col_start = lax.axis_index("seq") * w_attn_out.shape[1]
     attn_term = lax.dynamic_update_slice(
         jnp.zeros((batch_rows, model_width), jnp.float32), attn_cols, (jnp.int32(0), col_start)
     )
-    other_terms = mlp_term + attn_term
-    summed = ssm_summed + lax.psum_scatter(
-        other_terms, ("grp", "seq"), scatter_dimension=1, tiled=True
-    )
+    summed = scatter_sum(mlp_term + attn_term + ssm_term)
     hidden_out = (hidden_f + summed).astype(jnp.bfloat16)
     return (hidden_out, state_out)
 

time: 290 us -> 88 us (0.30)
  waiting for transfers between devices: 137 us -> 4.93 us
  blocking collectives: 89.5 us -> 13.4 us
  starting transfers between devices: 0.04 us -> 18.5 us
  between operations: 14.3 us -> 0.93 us
    reduce_scatter x1 -> x0, waiting for transfers between devices: 137 us -> none  [per_device(): lax.psum_scatter(ssm_term, ('grp', 'seq'), scatter_dimension=1, tiled=True)]
    all_gather x2 -> x0, blocking collectives: 51.2 us -> none  [the longest x1 44.2 us: per_device(): lax.all_gather(hidden_in, ('grp', 'seq'), axis=1, tiled=True)]
    psum x1 -> x0, blocking collectives: 38.3 us -> none  [per_device(): lax.psum(jnp.dot(conv_out.astype(jnp.bfloat16), w_state_proj, preferred_e...]
    all_to_all x0 -> x1, blocking collectives: none -> 13.4 us  [scatter_sum(): lax.all_to_all(blocks, BOTH, 1, 1).astype(jnp.float32)]
    all_to_all x0 -> x2, starting transfers between devices: none -> 10.8 us  [the longest x1 7.33 us: gather_features(): blocks = lax.all_to_all(rows, BOTH, 0, 0)]
    ppermute x0 -> x5, starting transfers between devices: none -> 7.61 us  [exchange_sum(): lax.ppermute(value, BOTH, [(i, i ^ step) for i in range(count)])]
    ppermute x0 -> x5, waiting for transfers between devices: none -> 4.92 us  [exchange_sum(): lax.ppermute(value, BOTH, [(i, i ^ step) for i in range(count)])]
  transfers between devices with their start and end apart: 1 -> 7, of which waited for: 1 -> 2; matrix products, arithmetic and copies ran while one was open for 0% -> 38% of each run, Pallas kernels for 0% -> 0%
where the time goes in v1:
time: 88 us; the launch traced here: 87.5 us
  matrix products  33.6 us (38%)
  starting transfers between devices  18.5 us (21%)
  blocking collectives  13.4 us (15%)
  local copies, waits for them, and re-layouts  8.55 us (10%)
  other arithmetic  7.5 us (9%)
  waiting for transfers between devices  4.93 us (6%)
  between operations  0.93 us (1%)
    all_to_all x1, blocking collectives, scatter_sum(): lax.all_to_all(blocks, BOTH, 1, 1).astype(jnp.float32)  13.4 us
    dot_general x1, matrix products, per_device(): jnp.dot(flat_inputs, key_projection, preferred_element_type=jnp.float32)  9.81 us
    ppermute x5, starting transfers between devices, exchange_sum(): lax.ppermute(value, BOTH, [(i, i ^ step) for i in range(count)])  7.61 us
    all_to_all x1, starting transfers between devices, gather_features(): blocks = lax.all_to_all(rows, BOTH, 0, 0)  7.33 us
    dot_general x1, matrix products, per_device(): jnp.dot(flat_inputs, value_projection, preferred_element_type=jnp.float32)  6.5 us
    dot_general x1, matrix products, per_device(): jnp.dot(mlp_hidden, w_mlp_down, preferred_element_type=jnp.float32)  5.07 us
    ppermute x5, waiting for transfers between devices, exchange_sum(): lax.ppermute(value, BOTH, [(i, i ^ step) for i in range(count)])  4.92 us
    dot_general x1, local copies, waits for them, and re-layouts, per_device(): jnp.dot(flat_inputs, key_projection, preferred_element_type=jnp.float32)  4.1 us
  transfers between devices with their start and end apart: 7, of which 2 were waited for; matrix products, arithmetic and copies ran while one was open for 38% of the time, Pallas kernels for 0%

profile of v1, /device:TPU:0, one launch (start us, length us, event | category | flops | bytes accessed | tf_op | source)
XLA Modules:
  0.0 87.5 jit_solution(10130403454004555585)
XLA Ops:
  0.6 1.5 %broadcast_in_dim.18 = bf16[32,24,128]{2,1,0:T(8,128)(2,1)} broadcast(bf16[24,128]{1,0:T(8,128)(2,1)} %param.23), dimensions={1,2} | broadcast | bytes 202752 | tf_op jit(solution)/shard_map/broadcast_in_dim | solution.py:34
  2.2 7.3 %all-to-all-start = ((bf16[32,24,128]{2,1,0:T(8,128)(2,1)}), bf16[32,24,128]{2,1,0:T(8,128)(2,1)S(1)}, u32[]{:S(2)}, u32[]{:S(2)}) async-start(bf16[32,24,128]{2,1,0:T(8,128)(2,1)} %broadcast_in_dim.18), calls=%async_computation | async-start | bytes 393216 | tf_op jit(solution)/shard_map/all_to_all | solution.py:35
  9.6 6.5 %convolution_convert_fusion = bf16[1536,256]{1,0:T(8,128)(2,1)S(1)} fusion(bf16[1536,4096]{1,0:T(8,128)(2,1)} %bitcast.64, bf16[4096,256]{1,0:T(8,128)(2,1)S(1)} %copy-done), kind=kOutput, calls=%fused_computation.4 | convolution fusion | flops 3221618688 | bytes 15466496 | tf_op jit(solution)/shard_map/dot_general | solution.py:154
  16.1 1.1 %reshape.170 = bf16[3,512,2,128]{3,2,1,0:T(2,128)(2,1)} reshape(bf16[1536,256]{1,0:T(8,128)(2,1)S(1)} %convolution_convert_fusion) | data formatting | bytes 1572864 | tf_op jit(solution)/shard_map/reshape | solution.py:156
  17.1 4.1 %copy.40 = bf16[256,4096]{1,0:T(8,128)(2,1)} copy(bf16[256,4096]{0,1:T(8,128)(2,1)} %bitcast.53) | data formatting | bytes 4194304 | tf_op jit(solution)/shard_map/dot_general | solution.py:149
  21.3 9.8 %fusion = f32[3,512,2,128]{1,3,2,0:T(8,128)} fusion(bf16[2,128,4096,1]{2,1,0,3:T(8,128)(2,1)} %bitcast.54, bf16[3,512,4096]{2,1,0:T(8,128)(2,1)} %param.44), kind=kOutput, calls=%fused_computation | convolution fusion | flops 3221225472 | bytes 16252928 | tf_op jit(solution)/shard_map/dot_general | solution.py:149
  31.1 0.5 multiply_cosine_fusion
  32.0 2.6 %subtract_convert_fusion = (bf16[3,512,2,64]{1,3,2,0:T(8,128)(2,1)}, bf16[3,512,2,64]{1,3,2,0:T(8,128)(2,1)}) fusion(f32[3,512,2,128]{1,3,2,0:T(8,128)} %fusion, f32[3,512,64]{1,2,0:T(8,128)S(1)} %get-tuple-element.17, f32[3,512,64]{1,2,0:T(8,128)S(1)} %get-tuple-element.16), kind=kLoop, calls=%fused_computation.25 | loop fusion | flops 1572864 | bytes 3145728 | tf_op jit(solution)/shard_map/convert.6
  34.8 2.1 %fusion.25 = f32[3,256]{1,0:T(4,128)S(1)} fusion(bf16[4096,256]{1,0:T(8,128)(2,1)} %param.38, bf16[24,4096]{1,0:T(8,128)(2,1)S(1)} %fusion.17, s32[]{:T(128)S(6)} %select_n.19), kind=kOutput, calls=%fused_computation.51 | convolution fusion | flops 6291456 | bytes 2132996 | tf_op jit(solution)/shard_map/dot_general | solution.py:136
  37.0 0.4 fusion.10
  37.5 1.1 %fusion.50 = f32[24,448]{1,0:T(8,128)S(1)} fusion(bf16[24,4096]{1,0:T(8,128)(2,1)S(1)} %fusion.17, bf16[4096,448]{0,1:T(8,128)(2,1)S(1)} %copy-done.2), kind=kOutput, calls=%fused_computation.90 | convolution fusion | flops 88080384 | bytes 3909632 | tf_op jit(solution)/shard_map/dot_general | solution.py:115
  38.6 0.7 copy-done.1
  39.3 0.6 fusion.27
  40.1 2.1 %convolution_convert_fusion.1 = bf16[24,256]{1,0:T(8,128)(2,1)S(1)} fusion(bf16[24,4096]{1,0:T(8,128)(2,1)S(1)} %fusion.17, bf16[4096,256]{1,0:T(8,128)(2,1)} %param.25), kind=kOutput, calls=%fused_computation.14 | convolution fusion | flops 50337792 | bytes 2306048 | tf_op jit(solution)/shard_map/dot_general | solution.py:85
  42.5 0.3 collective-permute-start
  42.8 0.2 fusion.34
  43.0 1.5 %fusion.46 = (f32[3,2,2]{2,1,0:T(2,128)S(1)}, f32[3,2,2,512]{3,2,1,0:T(2,128)S(1)}) fusion(bf16[3,512,2,64]{1,3,2,0:T(8,128)(2,1)} %get-tuple-element.9, bf16[3,512,2,64]{1,3,2,0:T(8,128)(2,1)} %get-tuple-element.8, bf16[3,2,2,64]{3,2,1,0:T(2,128)(2,1)S(1)} %bitcast.63, bf16[3,2,2,64]{3,2,1,0:T(2,128)(2,1)S(1)} %bitcast.61, ...), kind=kOutput, calls=%fused_computation.87 | convolution fusion | flops 3170292 | bytes 815664 | tf_op jit(solution)/shard_map/bkgd,bpkd->bkgp/dot_general | solution.py:160
  44.7 1.7 %collective-permute-start.1 = (f32[24,288]{1,0:T(8,128)S(1)}, f32[24,288]{1,0:T(8,128)S(1)}, u32[]{:S(2)}, u32[]{:S(2)}) collective-permute-start(f32[24,288]{1,0:T(8,128)S(1)} %add.109), channel_id=1, source_target_pairs={{0,2},{1,3},{2,0},{3,1},{4,6},{5,7},{6,4},{7,5},{8,10},{9,11},{10,... | collective-permute-start | bytes 82952 | tf_op jit(solution)/shard_map/ppermute | solution.py:43
  46.4 2.3 %collective-permute-done.1 = f32[24,288]{1,0:T(8,128)S(1)} collective-permute-done((f32[24,288]{1,0:T(8,128)S(1)}, f32[24,288]{1,0:T(8,128)S(1)}, u32[]{:S(2)}, u32[]{:S(2)}) %collective-permute-start.1) | collective-permute-done | bytes 27680 | tf_op jit(solution)/shard_map/ppermute | solution.py:43
  48.7 1.6 %collective-permute-start.2 = (f32[24,288]{1,0:T(8,128)S(1)}, f32[24,288]{1,0:T(8,128)S(1)}, u32[]{:S(2)}, u32[]{:S(2)}) collective-permute-start(f32[24,288]{1,0:T(8,128)S(1)} %add.110), channel_id=1, source_target_pairs={{0,4},{1,5},{2,6},{3,7},{4,0},{5,1},{6,2},{7,3},{8,12},{9,13},{10,... | collective-permute-start | bytes 82952 | tf_op jit(solution)/shard_map/ppermute | solution.py:43
  50.4 0.3 fusion.9
  50.7 0.6 broadcast_in_dim.22
  51.3 3.5 %all-to-all-start.1 = ((bf16[8,3,512]{2,1,0:T(4,128)(2,1)}), bf16[8,3,512]{2,1,0:T(4,128)(2,1)S(1)}, u32[]{:S(2)}, u32[]{:S(2)}) async-start(bf16[8,3,512]{2,1,0:T(4,128)(2,1)} %broadcast_in_dim.22), calls=%async_computation.1 | async-start | bytes 65536 | tf_op jit(solution)/shard_map/all_to_all | solution.py:182
  54.9 1.5 %collective-permute-start.3 = (f32[24,288]{1,0:T(8,128)S(1)}, f32[24,288]{1,0:T(8,128)}, u32[]{:S(2)}, u32[]{:S(2)}) collective-permute-start(f32[24,288]{1,0:T(8,128)S(1)} %add.111), channel_id=1, source_target_pairs={{0,8},{1,9},{2,10},{3,11},{4,12},{5,13},{6,14},{7,15},{8,0},{9,1},... | collective-permute-start | bytes 82952 | tf_op jit(solution)/shard_map/ppermute | solution.py:43
  56.4 5.1 %fusion.6 = f32[24,4096]{1,0:T(8,128)S(1)} fusion(bf16[448,4096]{1,0:T(8,128)(2,1)} %param.43, bf16[24,4096]{1,0:T(8,128)(2,1)S(1)} %fusion.17, bf16[4096,448]{0,1:T(8,128)(2,1)} %param.42, f32[24,448]{1,0:T(8,128)S(1)} %fusion.50), kind=kOutput, calls=%fused_computation.10 | convolution fusion | flops 176225280 | bytes 7972864 | tf_op jit(solution)/shard_map/dot_general | solution.py:118
  61.6 0.8 add.112
  62.3 2.5 %collective-permute-start.4 = (f32[24,288]{1,0:T(8,128)S(1)}, f32[24,288]{1,0:T(8,128)S(1)}, u32[]{:S(2)}, u32[]{:S(2)}) collective-permute-start(f32[24,288]{1,0:T(8,128)S(1)} %add.112), channel_id=1, source_target_pairs={{0,16},{1,17},{2,18},{3,19},{4,20},{5,21},{6,22},{7,23},{8,24},{9,... | collective-permute-start | bytes 82952 | tf_op jit(solution)/shard_map/ppermute | solution.py:43
  65.0 2.6 %collective-permute-done.4 = f32[24,288]{1,0:T(8,128)S(1)} collective-permute-done((f32[24,288]{1,0:T(8,128)S(1)}, f32[24,288]{1,0:T(8,128)S(1)}, u32[]{:S(2)}, u32[]{:S(2)}) %collective-permute-start.4) | collective-permute-done | bytes 27680 | tf_op jit(solution)/shard_map/ppermute | solution.py:43
  67.9 1.9 %multiply_reduce_fusion = (f32[24,256]{1,0:T(8,128)S(1)}, f32[24,16,256]{2,1,0:T(8,128)}) fusion(f32[24,16]{1,0:T(8,128)S(1)} %get-tuple-element.11, f32[24,256]{1,0:T(8,128)S(1)} %divide_multiply_fusion, f32[24,16]{1,0:T(8,128)S(1)} %get-tuple-element.10, f32[24,256]{1,0:T(8,128)S(1)} %get-tuple-element.23, f32[24,16,256]{2,1,0:T(8,128)} %param.35, ...), kind=kLoop, calls=%fused_computation.35 | loop fusion | flops 681984 | bytes 904192 | tf_op jit(solution)/shard_map/reduce_sum | solution.py:112
  69.8 3.5 %fusion.3 = bf16[3,32,8,128]{3,2,1,0:T(8,128)(2,1)S(1)} fusion(f32[24,4096]{1,0:T(8,128)S(1)} %fusion.4, bf16[256,4096]{1,0:T(8,128)(2,1)} %param.36, f32[24,256]{1,0:T(8,128)S(1)} %get-tuple-element.2, f32[24,256]{1,0:T(8,128)S(1)} %divide_multiply_fusion, f32[256]{0:T(256)S(1)} %copy-done.14, bf16[24,4096]{1,0:T(8,128)(2,1)S(1)} %fusion.17, ...), kind=kOutput, calls=%fused_computation.5 | convolution fusion | flops 100909056 | bytes 5030912 | tf_op jit(solution)/shard_map/dot_general | solution.py:114
  73.4 13.4 %all_to_all.15 = bf16[24,32,128]{2,0,1:T(8,128)(2,1)S(1)} all-to-all(bf16[24,32,128]{2,0,1:T(8,128)(2,1)S(1)} %bitcast.55), channel_id=1, replica_groups=mesh['grp'=4,'seq'=8] {'grp','seq'}, dimensions={1} | all-to-all | bytes 393216 | tf_op jit(solution)/shard_map/all_to_all | solution.py:51
  86.9 0.6 add_convert_fusion.1
  (69 shorter events, 2.1 us)
Async XLA Ops:
  0.6 8.9 %copy-start = (bf16[4096,256]{1,0:T(8,128)(2,1)S(1)}, bf16[4096,256]{1,0:T(8,128)(2,1)}, u32[]{:S(2)}) copy-start(bf16[4096,256]{1,0:T(8,128)(2,1)} %param.39) | copy-start | bytes 6291460
  2.2 32.3 %all-to-all-start = ((bf16[32,24,128]{2,1,0:T(8,128)(2,1)}), bf16[32,24,128]{2,1,0:T(8,128)(2,1)S(1)}, u32[]{:S(2)}, u32[]{:S(2)}) async-start(bf16[32,24,128]{2,1,0:T(8,128)(2,1)} %broadcast_in_dim.18), calls=%async_computation | async-start | bytes 393216 | tf_op jit(solution)/shard_map/all_to_all | solution.py:35
  21.2 10.4 %copy-start.15 = (s32[24]{0:T(128)S(1)}, s32[24]{0:T(128)}, u32[]{:S(2)}) copy-start(s32[24]{0:T(128)} %param.45) | copy-start | bytes 292
  21.2 10.6 %copy-start.11 = (f32[4,256]{1,0:T(4,128)S(1)}, f32[4,256]{1,0:T(4,128)}, u32[]{:S(2)}) copy-start(f32[4,256]{1,0:T(4,128)} %param.27) | copy-start | bytes 12292
  21.3 10.6 %copy-start.10 = (f32[16,256]{1,0:T(8,128)S(1)}, f32[16,256]{1,0:T(8,128)}, u32[]{:S(2)}) copy-start(f32[16,256]{1,0:T(8,128)} %param.33) | copy-start | bytes 49156
  21.3 10.7 %copy-start.7 = (bf16[24,3,256]{2,0,1:T(8,128)(2,1)S(1)}, bf16[24,3,256]{2,0,1:T(8,128)(2,1)}, u32[]{:S(2)}) copy-start(bf16[24,3,256]{2,0,1:T(8,128)(2,1)} %param.29) | copy-start | bytes 110596
  31.1 3.6 %copy-start.9 = (f32[4096]{0:T(1024)S(1)}, f32[4096]{0:T(1024)}, u32[]{:S(2)}) copy-start(f32[4096]{0:T(1024)} %param.24) | copy-start | bytes 49156
  34.8 2.7 %copy-start.2 = (bf16[4096,448]{0,1:T(8,128)(2,1)S(1)}, bf16[4096,448]{0,1:T(8,128)(2,1)}, u32[]{:S(2)}) copy-start(bf16[4096,448]{0,1:T(8,128)(2,1)} %param.41) | copy-start | bytes 11010052
  37.0 2.3 %copy-start.1 = (bf16[4096,512]{1,0:T(8,128)(2,1)S(1)}, bf16[4096,512]{1,0:T(8,128)(2,1)}, u32[]{:S(2)}) copy-start(bf16[4096,512]{1,0:T(8,128)(2,1)} %param.37) | copy-start | bytes 12582916
  39.9 2.3 %copy-start.12 = (f32[256]{0:T(256)S(1)}, f32[256]{0:T(256)}, u32[]{:S(2)}) copy-start(f32[256]{0:T(256)} %param.28) | copy-start | bytes 3076
  39.9 2.4 %copy-start.5 = (bf16[256,288]{0,1:T(8,128)(2,1)S(1)}, bf16[256,288]{0,1:T(8,128)(2,1)}, u32[]{:S(2)}) copy-start(bf16[256,288]{0,1:T(8,128)(2,1)} %param.30) | copy-start | bytes 442372
  40.0 10.4 %copy-start.3 = (bf16[3,512,2,128]{3,2,1,0:T(2,128)(2,1)S(1)}, bf16[3,512,2,128]{3,2,1,0:T(2,128)(2,1)}, u32[]{:S(2)}) copy-start(bf16[3,512,2,128]{3,2,1,0:T(2,128)(2,1)} %reshape.170) | copy-start | bytes 2359300
  42.5 2.2 %collective-permute-start = (f32[24,288]{1,0:T(8,128)S(1)}, f32[24,288]{1,0:T(8,128)S(1)}, u32[]{:S(2)}, u32[]{:S(2)}) collective-permute-start(f32[24,288]{1,0:T(8,128)S(1)} %fusion.30), channel_id=1, source_target_pairs={{0,1},{1,0},{2,3},{3,2},{4,5},{5,4},{6,7},{7,6},{8,9},{9,8},{10,11... | collective-permute-start | bytes 82952 | tf_op jit(solution)/shard_map/ppermute | solution.py:43
  44.7 4.0 %collective-permute-start.1 = (f32[24,288]{1,0:T(8,128)S(1)}, f32[24,288]{1,0:T(8,128)S(1)}, u32[]{:S(2)}, u32[]{:S(2)}) collective-permute-start(f32[24,288]{1,0:T(8,128)S(1)} %add.109), channel_id=1, source_target_pairs={{0,2},{1,3},{2,0},{3,1},{4,6},{5,7},{6,4},{7,5},{8,10},{9,11},{10,... | collective-permute-start | bytes 82952 | tf_op jit(solution)/shard_map/ppermute | solution.py:43
  48.7 6.1 %collective-permute-start.2 = (f32[24,288]{1,0:T(8,128)S(1)}, f32[24,288]{1,0:T(8,128)S(1)}, u32[]{:S(2)}, u32[]{:S(2)}) collective-permute-start(f32[24,288]{1,0:T(8,128)S(1)} %add.110), channel_id=1, source_target_pairs={{0,4},{1,5},{2,6},{3,7},{4,0},{5,1},{6,2},{7,3},{8,12},{9,13},{10,... | collective-permute-start | bytes 82952 | tf_op jit(solution)/shard_map/ppermute | solution.py:43
  51.3 10.2 %all-to-all-start.1 = ((bf16[8,3,512]{2,1,0:T(4,128)(2,1)}), bf16[8,3,512]{2,1,0:T(4,128)(2,1)S(1)}, u32[]{:S(2)}, u32[]{:S(2)}) async-start(bf16[8,3,512]{2,1,0:T(4,128)(2,1)} %broadcast_in_dim.22), calls=%async_computation.1 | async-start | bytes 65536 | tf_op jit(solution)/shard_map/all_to_all | solution.py:182
  54.9 9.9 %copy-start.4 = (bf16[512,512]{1,0:T(8,128)(2,1)S(1)}, bf16[512,512]{1,0:T(8,128)(2,1)}, u32[]{:S(2)}) copy-start(bf16[512,512]{1,0:T(8,128)(2,1)} %param.40) | copy-start | bytes 1572868
  54.9 12.8 %copy-start.6 = (bf16[256,256]{1,0:T(8,128)(2,1)S(1)}, bf16[256,256]{1,0:T(8,128)(2,1)}, u32[]{:S(2)}) copy-start(bf16[256,256]{1,0:T(8,128)(2,1)} %param.31) | copy-start | bytes 393220
  54.9 12.8 %copy-start.13 = (f32[256]{0:T(256)S(1)}, f32[256]{0:T(256)}, u32[]{:S(2)}) copy-start(f32[256]{0:T(256)} %param.32) | copy-start | bytes 3076
  54.9 6.7 %collective-permute-start.3 = (f32[24,288]{1,0:T(8,128)S(1)}, f32[24,288]{1,0:T(8,128)}, u32[]{:S(2)}, u32[]{:S(2)}) collective-permute-start(f32[24,288]{1,0:T(8,128)S(1)} %add.111), channel_id=1, source_target_pairs={{0,8},{1,9},{2,10},{3,11},{4,12},{5,13},{6,14},{7,15},{8,0},{9,1},... | collective-permute-start | bytes 82952 | tf_op jit(solution)/shard_map/ppermute | solution.py:43
  61.5 8.3 %copy-start.14 = (f32[256]{0:T(256)S(1)}, f32[256]{0:T(256)}, u32[]{:S(2)}) copy-start(f32[256]{0:T(256)} %param.34) | copy-start | bytes 3076
  62.3 5.2 %collective-permute-start.4 = (f32[24,288]{1,0:T(8,128)S(1)}, f32[24,288]{1,0:T(8,128)S(1)}, u32[]{:S(2)}, u32[]{:S(2)}) collective-permute-start(f32[24,288]{1,0:T(8,128)S(1)} %add.112), channel_id=1, source_target_pairs={{0,16},{1,17},{2,18},{3,19},{4,20},{5,21},{6,22},{7,23},{8,24},{9,... | collective-permute-start | bytes 82952 | tf_op jit(solution)/shard_map/ppermute | solution.py:43
  69.8 17.1 %copy-start.8 = (bf16[24,128]{1,0:T(8,128)(2,1)S(1)}, bf16[24,128]{1,0:T(8,128)(2,1)}, u32[]{:S(2)}) copy-start(bf16[24,128]{1,0:T(8,128)(2,1)} %param.23) | copy-start | bytes 18436
